TPU v7x, 32 devices: a whole 2x2x4 slice. The times are simulated.
32 devices in a mesh: blk: 8 (over z, x), grp: 4 (over y, core).
Axes of the slice: x: 2, y: 2, z: 4, core: 2. Of those that a mesh axis runs over, the one named last changes fastest.
Arguments:
- coil_pos: float32 [3, 1280], P(None, ('blk', 'grp')), may hold values from -1 to 1
- coil_radius: float32 [1280], P(('blk', 'grp')), may hold values from 0.02 to 0.08
- coil_current: bfloat16 [64, 1280], P(None, ('blk', 'grp')), may hold values from -0.3125 to 0.3125
- blank_pos: float32 [3, 4096], P(None, ('blk', 'grp')), may hold values from -1 to 1
- blank_rule: int32 [4096], P(('blk', 'grp')), may hold values from 0 to 7
- blank_cond: float32 [4096], P(('blk', 'grp')), may hold values from 0.3 to 3
- quad_offset: float32 [3, 8, 2], replicated, may hold values from -0.1 to 0.1
- quad_weight: float32 [8, 2], replicated, may hold values from 0.3 to 0.7
Outputs:
- blank_current: bfloat16 [64, 4096], P(None, ('blk', 'grp'))
- coil_reaction: float32 [64, 1280], P(None, ('blk', 'grp'))
All inputs are finite; a program needn't handle non-finite values.
Results may differ from a plain program's by a relative error of at most 0.0066.
Values may be sent and summed in bfloat16 or wider, within the bound.
A program may use at most 64 MiB of HBM per device.

v0:
```python
import math
import jax
import jax.numpy as jnp
from jax import lax
from jax.sharding import PartitionSpec as P


def blank_geometry(blank_pos, blank_rule, quad_offset, quad_weight):
    rules = quad_weight.shape[0]
    points = quad_weight.shape[1]
    onehot = (blank_rule[None, :] == jnp.arange(rules, dtype=jnp.int32)[:, None]).astype(
        jnp.float32
    )
    table_rows = []
    base_rows = []
    zeros_row = jnp.zeros_like(blank_pos[0])
    for point in range(points):
        table_rows += [
            quad_offset[0, :, point],
            quad_offset[1, :, point],
            quad_offset[2, :, point],
            quad_weight[:, point],
        ]
        base_rows += [blank_pos[0], blank_pos[1], blank_pos[2], zeros_row]
    table = jnp.stack(table_rows, 0)
    base = jnp.stack(base_rows, 0)
    return base + jnp.dot(table, onehot, precision=lax.Precision.HIGHEST)


def kernel_block(coil_geometry, geometry):
    points = geometry.shape[0] // 4
    running = jnp.zeros((coil_geometry.shape[1], geometry.shape[1]), jnp.float32)
    for point in range(points):
        delta_x = coil_geometry[0][:, None] - geometry[4 * point][None, :]
        delta_y = coil_geometry[1][:, None] - geometry[4 * point + 1][None, :]
        delta_z = coil_geometry[2][:, None] - geometry[4 * point + 2][None, :]
        squared = (
            delta_x * delta_x + delta_y * delta_y + delta_z * delta_z + coil_geometry[3][:, None]
        )
        running = running + geometry[4 * point + 3][None, :] * lax.rsqrt(squared)
    return running


def blockwise(width, limit, step_fn, initial):
    block = math.gcd(width, limit)
    count = width // block

    def advance(index, carried):
        start = (index * block).astype(jnp.int32)
        return step_fn(carried, start, block)

    return lax.fori_loop(0, count, advance, initial)


def per_device(
    coil_pos, coil_radius, coil_current, blank_pos, blank_rule, blank_cond, quad_offset, quad_weight
):
    coil_geometry = jnp.concatenate([coil_pos, (coil_radius * coil_radius)[None, :]], 0)
    geometry = blank_geometry(blank_pos, blank_rule, quad_offset, quad_weight)
    samples = coil_current.shape[0]
    coil_count = coil_current.shape[1]
    local_blanks = geometry.shape[1]
    total_blanks = local_blanks * lax.axis_size("blk") * lax.axis_size("grp")
    all_current = lax.all_gather(coil_current, ("blk", "grp"), axis=1, tiled=True)
    portion = lax.all_gather(coil_geometry, ("blk", "grp"), axis=1, tiled=True)

    def collect_inner(carried, start, block):
        rows = lax.dynamic_slice_in_dim(portion, start, block, 1)
        kernel_tile = kernel_block(rows, geometry).astype(jnp.bfloat16)
        currents = lax.dynamic_slice_in_dim(all_current, start, block, 1)
        return carried + jnp.dot(currents, kernel_tile, preferred_element_type=jnp.float32)

    induced = blockwise(
        portion.shape[1], 2048, collect_inner, jnp.zeros((samples, local_blanks), jnp.float32)
    )
    blank_current = induced.astype(jnp.bfloat16)
    weighted = (blank_cond[None, :] * blank_current.astype(jnp.float32)).astype(jnp.bfloat16)
    all_weighted = lax.all_gather(weighted, ("blk", "grp"), axis=1, tiled=True)
    reflect_portion = lax.all_gather(geometry, ("blk", "grp"), axis=1, tiled=True)

    def reflect_inner(carried, start, block):
        columns = lax.dynamic_slice_in_dim(reflect_portion, start, block, 1)
        kernel_tile = kernel_block(coil_geometry, columns).astype(jnp.bfloat16)
        currents = lax.dynamic_slice_in_dim(all_weighted, start, block, 1)
        return carried + lax.dot_general(
            currents, kernel_tile, (((1,), (1,)), ((), ())), preferred_element_type=jnp.float32
        )

    reaction = blockwise(
        reflect_portion.shape[1], 2048, reflect_inner, jnp.zeros((samples, coil_count), jnp.float32)
    )
    coil_reaction = reaction * (2.0 / total_blanks)
    return (blank_current, coil_reaction)


def solution(mesh):
    in_specs = (
        P(None, ("blk", "grp")),
        P(("blk", "grp")),
        P(None, ("blk", "grp")),
        P(None, ("blk", "grp")),
        P(("blk", "grp")),
        P(("blk", "grp")),
        P(),
        P(),
    )
    out_specs = (P(None, ("blk", "grp")), P(None, ("blk", "grp")))
    return jax.shard_map(
        per_device, mesh=mesh, in_specs=in_specs, out_specs=out_specs, check_vma=False
    )
```

profile of v0, /device:TPU:0, one launch (start us, length us, event | category | flops | bytes accessed | tf_op | source)
XLA Modules:
  0.0 166.7 jit_solution(2309037192950104632)
XLA Ops:
  0.6 0.0 copy-start.7
  0.6 0.6 copy-done.7
  1.3 0.0 copy-start.4
  1.3 0.7 copy-done.4
  2.0 0.0 copy-start
  2.0 0.0 copy-start.2
  2.0 0.7 copy-done
  2.7 0.0 copy-done.2
  2.7 0.0 copy-start.3
  2.7 0.0 copy-start.6
  2.7 0.6 copy-done.3
  3.4 0.0 copy-done.6
  3.4 0.1 convolution_add_fusion.2
  3.5 43.4 %all-gather = f32[32,40,4]{1,2,0:T(4,128)S(1)} all-gather(f32[1,40,4]{1,2,0:T(4,128)S(1)} %maximum_bitcast_fusion), channel_id=1, replica_groups=mesh['blk'=8,'grp'=4] {'blk','grp'}, dimensions={0}, use_global_device_ids=true | all-gather | bytes 21120 | tf_op jit(solution)/shard_map/all_gather | solution.py:65
  46.9 0.1 reshape.15
  47.0 0.0 copy-start.1
  47.0 37.0 %all_gather.15 = f32[8,4096]{1,0:T(8,128)S(1)} all-gather(f32[8,128]{1,0:T(8,128)S(1)} %convolution_add_fusion.2), channel_id=1, replica_groups=mesh['blk'=8,'grp'=4] {'blk','grp'}, dimensions={1}, use_global_device_ids=true | all-gather | bytes 135168 | tf_op jit(solution)/shard_map/all_gather | solution.py:79
  84.0 0.0 copy-done.1
  84.0 38.8 %all_gather.12 = bf16[64,1280]{0,1:T(8,128)(2,1)S(1)} all-gather(bf16[64,40]{0,1:T(8,128)(2,1)S(1)} %copy-done.1), channel_id=1, replica_groups=mesh['blk'=8,'grp'=4] {'blk','grp'}, dimensions={1}, use_global_device_ids=true | all-gather | bytes 168960 | tf_op jit(solution)/shard_map/all_gather | solution.py:64
  122.9 0.2 copy.14
  123.0 2.3 %while.28 = (s32[]{:T(128)}, f32[64,128]{1,0:T(8,128)S(1)}, bf16[64,1280]{1,0:T(8,128)(2,1)S(1)}, f32[8,128]{1,0:T(8,128)S(1)}, f32[4,1280]{1,0:T(4,128)S(1)}, /...) while((s32[]{:T(128)}, f32[64,128]{1,0:T(8,128)S(1)}, ...), condition=%wide.region_1.0_spmd.clone, body=%wide.region_0.0_spmd.clone.sunk | while | flops 4931594 | bytes 123117 | solution.py:52
  123.1 0.1 constant_dynamic-slice_fusion.3
  123.1 0.3 convolution_add_fusion.5
  123.5 0.1 constant_dynamic-slice_fusion.3
  123.6 0.3 convolution_add_fusion.5
  124.0 0.1 constant_dynamic-slice_fusion.3
  124.1 0.3 convolution_add_fusion.5
  124.4 0.1 constant_dynamic-slice_fusion.3
  124.5 0.3 convolution_add_fusion.5
  124.9 0.1 constant_dynamic-slice_fusion.3
  125.0 0.3 convolution_add_fusion.5
  125.4 0.0 copy-start.5
  125.4 0.6 copy-done.5
  126.0 0.6 multiply_convert_fusion
  126.6 38.0 %all_gather.14 = bf16[64,4096]{1,0:T(8,128)(2,1)S(1)} all-gather(bf16[64,128]{1,0:T(8,128)(2,1)S(1)} %get-tuple-element.278), channel_id=1, replica_groups=mesh['blk'=8,'grp'=4] {'blk','grp'}, dimensions={1}, use_global_device_ids=true | all-gather | bytes 540672 | tf_op jit(solution)/shard_map/all_gather | solution.py:78
  164.7 1.4 while.29
  164.7 0.2 fusion.36
  164.9 0.5 convolution_add_fusion.6
  165.4 0.2 fusion.36
  165.6 0.5 convolution_add_fusion.6
  166.0 0.6 broadcast_multiply_fusion
  (16 shorter events, 0.1 us)
Async XLA Ops:
  0.6 0.7 copy-start.7
  1.3 0.7 copy-start.4
  2.0 0.7 copy-start
  2.0 0.7 copy-start.2
  2.7 0.7 copy-start.3
  2.7 0.7 copy-start.6
  47.0 37.0 %copy-start.1 = (bf16[64,40]{0,1:T(8,128)(2,1)S(1)}, bf16[64,40]{0,1:T(8,128)(2,1)}, u32[]{:S(2)}) copy-start(bf16[64,40]{0,1:T(8,128)(2,1)} %param.14) | copy-start | bytes 15364
  125.4 0.7 copy-start.5
where the time goes:
time: 167 us
  blocking collectives  157 us (94%)
  local copies, waits for them, and re-layouts  4.47 us (3%)
  matrix products  2.78 us (2%)
    all_gather x1, blocking collectives, per_device(): portion = lax.all_gather(coil_geometry, ('blk', 'grp'), axis=1, tiled=True)  43.4 us
    all_gather x1, blocking collectives, per_device(): lax.all_gather(coil_current, ('blk', 'grp'), axis=1, tiled=True)  38.8 us
    all_gather x1, blocking collectives, per_device(): all_weighted = lax.all_gather(weighted, ('blk', 'grp'), axis=1, tiled=True)  38 us
    all_gather x1, blocking collectives, per_device(): lax.all_gather(geometry, ('blk', 'grp'), axis=1, tiled=True)  37 us
    unnamed x18, local copies, waits for them, and re-layouts  3.58 us

commit v1 on v0

--- a/solution.py
+++ b/solution.py
@@ -3,6 +3,14 @@
 import jax.numpy as jnp
 from jax import lax
 from jax.sharding import PartitionSpec as P
+
+start_samples_all = lambda frame_in, sheet: jnp.split(
+    lax.all_gather(
+        jnp.concatenate([frame_in, sheet], axis=0), axis_name=("blk", "grp"), axis=1, tiled=True
+    ),
+    [frame_in.shape[0]],
+    axis=0,
+)
 
 
 def blank_geometry(blank_pos, blank_rule, quad_offset, quad_weight):
@@ -61,8 +69,7 @@
     coil_count = coil_current.shape[1]
     local_blanks = geometry.shape[1]
     total_blanks = local_blanks * lax.axis_size("blk") * lax.axis_size("grp")
-    all_current = lax.all_gather(coil_current, ("blk", "grp"), axis=1, tiled=True)
-    portion = lax.all_gather(coil_geometry, ("blk", "grp"), axis=1, tiled=True)
+    all_current, portion = start_samples_all(coil_current, coil_geometry)
 
     def collect_inner(carried, start, block):
         rows = lax.dynamic_slice_in_dim(portion, start, block, 1)

time: 167 us -> 133 us (0.80)
  blocking collectives: 157 us -> 121 us
  local copies, waits for them, and re-layouts: 4.47 us -> 6.28 us
    all_gather x2 -> x1, blocking collectives: 82.2 us -> 45 us  [lax.all_gather(jnp.concatenate([frame_in, sheet], axis=0), axis_name=('bl...]
    unnamed x18 -> x17, local copies, waits for them, and re-layouts: 3.58 us -> 4.27 us
where the time goes in v1:
time: 133 us
  blocking collectives  121 us (91%)
  local copies, waits for them, and re-layouts  6.28 us (5%)
  matrix products  2.77 us (2%)
    all_gather x1, blocking collectives, lax.all_gather(jnp.concatenate([frame_in, sheet], axis=0), axis_name=('bl...  45 us
    all_gather x1, blocking collectives, per_device(): lax.all_gather(geometry, ('blk', 'grp'), axis=1, tiled=True)  38.3 us
    all_gather x1, blocking collectives, per_device(): all_weighted = lax.all_gather(weighted, ('blk', 'grp'), axis=1, tiled=True)  38 us
    unnamed x17, local copies, waits for them, and re-layouts  4.27 us

profile of v1, /device:TPU:0, one launch (start us, length us, event | category | flops | bytes accessed | tf_op | source)
XLA Modules:
  0.0 132.6 jit_solution(15322224333912718725)
XLA Ops:
  0.6 0.8 slice_bitcast_fusion.12
  1.4 0.0 copy-start.3
  1.4 0.7 copy-done.3
  2.1 0.0 copy-start.2
  2.1 0.0 copy-start.5
  2.1 0.6 copy-done.2
  2.8 0.0 copy-done.5
  2.8 0.0 copy-start.6
  2.8 0.1 convolution_add_fusion.2
  2.9 0.5 copy-done.6
  3.4 0.0 copy-start.1
  3.4 0.1 copy.12
  3.5 0.6 copy-done.1
  4.1 0.0 copy-start
  4.1 0.7 copy-done
  4.8 0.1 copy.11
  4.9 0.1 pad_maximum_fusion
  5.0 45.0 %all_gather.9 = f32[68,1280]{0,1:T(8,128)S(1)} all-gather(f32[68,40]{0,1:T(8,128)S(1)} %pad_maximum_fusion), channel_id=1, replica_groups=mesh['blk'=8,'grp'=4] {'blk','grp'}, dimensions={1}, use_global_device_ids=true | all-gather | bytes 359040 | tf_op jit(solution)/shard_map/all_gather | solution.py:8
  50.0 0.2 split.9
  50.2 0.2 copy.14
  50.5 0.2 copy.13
  50.7 2.3 %while.28 = (s32[]{:T(128)}, f32[64,128]{1,0:T(8,128)S(1)}, bf16[64,1280]{1,0:T(8,128)(2,1)S(1)}, f32[8,128]{1,0:T(8,128)S(1)}, f32[4,1280]{1,0:T(4,128)S(1)}, /...) while((s32[]{:T(128)}, f32[64,128]{1,0:T(8,128)S(1)}, ...), condition=%wide.region_1.0_spmd.clone, body=%wide.region_0.0_spmd.clone.sunk | while | flops 4931594 | bytes 123109 | solution.py:60
  50.7 0.1 constant_dynamic-slice_fusion.3
  50.8 0.3 convolution_add_fusion.5
  51.2 0.1 constant_dynamic-slice_fusion.3
  51.3 0.3 convolution_add_fusion.5
  51.6 0.1 constant_dynamic-slice_fusion.3
  51.7 0.3 convolution_add_fusion.5
  52.1 0.1 constant_dynamic-slice_fusion.3
  52.2 0.3 convolution_add_fusion.5
  52.6 0.1 constant_dynamic-slice_fusion.3
  52.7 0.3 convolution_add_fusion.5
  53.0 0.0 copy-start.4
  53.0 0.6 copy-done.4
  53.7 0.6 multiply_convert_fusion
  54.3 38.0 %all_gather.10 = bf16[64,4096]{1,0:T(8,128)(2,1)S(1)} all-gather(bf16[64,128]{1,0:T(8,128)(2,1)S(1)} %get-tuple-element.273), channel_id=1, replica_groups=mesh['blk'=8,'grp'=4] {'blk','grp'}, dimensions={1}, use_global_device_ids=true | all-gather | bytes 540672 | tf_op jit(solution)/shard_map/all_gather | solution.py:85
  92.3 38.3 %all_gather.11 = f32[8,4096]{1,0:T(8,128)S(1)} all-gather(f32[8,128]{1,0:T(8,128)S(1)} %get-tuple-element.509), channel_id=1, replica_groups=mesh['blk'=8,'grp'=4] {'blk','grp'}, dimensions={1}, use_global_device_ids=true | all-gather | bytes 135168 | tf_op jit(solution)/shard_map/all_gather | solution.py:86
  130.6 1.4 %while.29 = (s32[]{:T(128)}, f32[64,40]{0,1:T(8,128)S(1)}, bf16[64,4096]{1,0:T(8,128)(2,1)S(1)}, f32[8,4096]{1,0:T(8,128)S(1)}, f32[3,40]{1,0:T(4,128)S(1)}, /*i...) while((s32[]{:T(128)}, f32[64,40]{0,1:T(8,128)S(1)}, ...), condition=%wide.region_3.0_spmd.clone, body=%wide.region_2.0_spmd.clone.sunk | while | flops 12293134 | bytes 492813 | solution.py:60
  130.6 0.2 fusion.36
  130.8 0.5 convolution_add_fusion.6
  131.3 0.2 fusion.36
  131.5 0.5 convolution_add_fusion.6
  132.0 0.6 broadcast_multiply_fusion
  (15 shorter events, 0.1 us)
Async XLA Ops:
  1.4 0.7 copy-start.3
  2.1 0.7 copy-start.2
  2.1 0.7 copy-start.5
  2.8 0.7 copy-start.6
  3.4 0.7 copy-start.1
  4.1 0.7 copy-start
  53.0 0.7 copy-start.4
